TPU v7x, 32 devices: a whole 2x2x4 slice. The times are simulated.
32 devices in a mesh: dp: 2 (over x), tp: 16 (over z, y, core).
Axes of the slice: x: 2, y: 2, z: 4, core: 2. Of those that a mesh axis runs over, the one named last changes fastest.
Arguments:
- query_hidden: bfloat16 [128, 8, 1024], P(('dp', 'tp')), parts along dimension 0
- doc_hidden: bfloat16 [128, 48, 1024], P(('dp', 'tp')), parts along dimension 0
- query_mask: int32 [128, 8], P(('dp', 'tp')), parts along dimension 0
- doc_mask: int32 [128, 48], P(('dp', 'tp')), parts along dimension 0
- positives: int32 [128], P(('dp', 'tp')), parts along dimension 0
- head_weight: bfloat16 [1024, 32768], P(None, 'tp')
- head_bias: float32 [1, 32768], P(None, 'tp')
Outputs:
- output 1: float32 [2], P('dp'), parts along dimension 0
- output 2: bfloat16 [2048, 32768], P('dp', 'tp'), parts along dimension 0
- output 3: float32 [2, 32768], P('dp', 'tp'), parts along dimension 0
- output 4: bfloat16 [128, 8, 1024], P(('dp', 'tp')), parts along dimension 0
- output 5: bfloat16 [128, 48, 1024], P(('dp', 'tp')), parts along dimension 0
There are 2 independent parts. A program takes and returns all parts, laid end to end along the dimension named above; an argument that names none is the same for every part.
All inputs are finite; a program needn't handle non-finite values.
Results may differ from a plain program's by a relative error of at most 0.010234.
Values are sent between devices in bfloat16 or wider.
A program may use at most 1 GiB of HBM per device.

v0:
```python
import math
import jax
import jax.numpy as jnp
from jax import lax
from jax.sharding import PartitionSpec as P

FULL_PRECISION = lax.Precision.HIGHEST


def head_forward(hidden, token_mask, head_weight, head_bias):
    logits = jnp.einsum('blh,hv->blv', hidden, head_weight, preferred_element_type=jnp.float32) + head_bias
    keep_mask = token_mask[:, :, None].astype(jnp.float32)
    return logits, jnp.sum(jnp.log1p(jnp.maximum(logits, 0.0)) * keep_mask, axis=1)


def head_backward(hidden, token_mask, head_weight, logits, grad_rep):
    keep_mask = token_mask[:, :, None].astype(jnp.float32)
    grad_gate = jnp.where(logits > 0.0, 1.0 / (1.0 + logits), 0.0) * keep_mask
    grad_logits = grad_rep[:, None, :] * grad_gate
    bias_part = jnp.sum(grad_logits, axis=(0, 1))
    grad_low = grad_logits.astype(jnp.bfloat16)
    weight_part = jnp.einsum('blh,blv->hv', hidden, grad_low, preferred_element_type=jnp.float32)
    hidden_part = jnp.einsum('blv,hv->blh', grad_low, head_weight, preferred_element_type=jnp.float32)
    return weight_part, bias_part, hidden_part.astype(jnp.bfloat16)


def solution(mesh):
    group_size = mesh.shape['tp']

    def device_step(query_hidden, doc_hidden, query_mask, doc_mask, positives, head_weight, head_bias):
        vocab_size = head_weight.shape[1] * group_size
        q_len = query_hidden.shape[1]
        d_len = doc_hidden.shape[1]
        query_weight = math.sqrt(d_len) / (4.0 * math.sqrt(vocab_size) * q_len)
        doc_weight = q_len / (4.0 * math.sqrt(vocab_size) * d_len ** 1.5)
        hid_q = lax.all_gather(query_hidden, 'tp', axis=0, tiled=True)
        hid_d = lax.all_gather(doc_hidden, 'tp', axis=0, tiled=True)
        keep_q = lax.all_gather(query_mask, 'tp', axis=0, tiled=True)
        keep_d = lax.all_gather(doc_mask, 'tp', axis=0, tiled=True)
        pos_all = lax.all_gather(positives, 'tp', axis=0, tiled=True)
        logits_q, rep_q = head_forward(hid_q, keep_q, head_weight, head_bias)
        logits_d, rep_d = head_forward(hid_d, keep_d, head_weight, head_bias)
        n_query = rep_q.shape[0]
        n_doc = rep_d.shape[0]
        mean_q = jnp.mean(rep_q, axis=0)
        mean_d = jnp.mean(rep_d, axis=0)
        score_part = jnp.einsum('qv,kv->qk', rep_q, rep_d, precision=FULL_PRECISION, preferred_element_type=jnp.float32)
        reg_part = query_weight * jnp.sum(mean_q * mean_q) + doc_weight * jnp.sum(mean_d * mean_d)
        scores, reg_total = lax.psum((score_part, reg_part), 'tp')
        log_norm = jax.nn.logsumexp(scores, axis=1)
        target = pos_all[:, None] == jnp.arange(n_doc)[None, :]
        picked = jnp.sum(jnp.where(target, scores, 0.0), axis=1)
        total_loss = jnp.mean(log_norm - picked) + reg_total
        grad_scores = (jnp.exp(scores - log_norm[:, None]) - target.astype(jnp.float32)) / n_query
        grad_q = jnp.einsum('qk,kv->qv', grad_scores, rep_d, precision=FULL_PRECISION, preferred_element_type=jnp.float32) + (2.0 * query_weight / n_query) * mean_q
        grad_d = jnp.einsum('qk,qv->kv', grad_scores, rep_q, precision=FULL_PRECISION, preferred_element_type=jnp.float32) + (2.0 * doc_weight / n_doc) * mean_d
        weight_q, bias_q, hidden_q = head_backward(hid_q, keep_q, head_weight, logits_q, grad_q)
        weight_d, bias_d, hidden_d = head_backward(hid_d, keep_d, head_weight, logits_d, grad_d)
        grad_query = lax.psum_scatter(hidden_q, 'tp', scatter_dimension=0, tiled=True)
        grad_doc = lax.psum_scatter(hidden_d, 'tp', scatter_dimension=0, tiled=True)
        grad_weight = (weight_q + weight_d).astype(jnp.bfloat16)
        grad_bias = (bias_q + bias_d)[None, :]
        return total_loss.reshape(1), grad_weight, grad_bias, grad_query, grad_doc

    batch_rows = P(('dp', 'tp'), None, None)
    batch_masks = P(('dp', 'tp'), None)
    return jax.shard_map(device_step, mesh=mesh, in_specs=(batch_rows, batch_rows, batch_masks, batch_masks, P(('dp', 'tp')), P(None, 'tp'), P(None, 'tp')), out_specs=(P('dp'), P('dp', 'tp'), P('dp', 'tp'), batch_rows, batch_rows), check_vma=False)
```

profile of v0, /device:TPU:0, one launch (start us, length us, event | category | flops | bytes accessed | tf_op | source)
XLA Modules:
  0.0 366.2 jit_solution(3700271614293214870)
XLA Ops:
  7.2 0.0 all-gather.5.cloned.1.call-start
  7.2 0.7 all-gather.5.cloned.1.call-update
  7.9 0.0 all-gather.7.cloned.1.call-start
  7.9 0.7 all-gather.7.cloned.1.call-update
  8.6 0.0 reduce-scatter.3.cloned.1.call-start
  8.7 23.2 %all-gather = s32[16,4,8]{2,1,0:T(4,128)S(1)} all-gather(s32[1,4,8]{2,1,0:T(4,128)} %bitcast.62), channel_id=1, replica_groups=mesh['dp'=2,'tp'=16] {'tp'}, dimensions={0}, use_global_device_ids=true | all-gather | bytes 2176 | tf_op jit(solution)/shard_map/all_gather | solution.py:38
  31.9 0.0 copy-start.1
  32.0 17.5 %all-gather.1 = s32[16,4,48]{2,1,0:T(4,128)S(1)} all-gather(s32[1,4,48]{2,1,0:T(4,128)} %bitcast.63), channel_id=1, replica_groups=mesh['dp'=2,'tp'=16] {'tp'}, dimensions={0}, use_global_device_ids=true | all-gather | bytes 13056 | tf_op jit(solution)/shard_map/all_gather | solution.py:39
  49.5 1.2 dynamic-slice
  51.4 0.9 dynamic-update-slice
  52.3 9.4 %all-reduce = s32[64]{0:T(128)S(1)} all-reduce(s32[64]{0:T(128)S(1)} %dynamic-update-slice), channel_id=1, replica_groups=mesh['dp'=2,'tp'=16] {'tp'}, use_global_device_ids=true, to_apply=%add | all-reduce | flops 64 | bytes 512
  61.6 0.0 all-gather.5.cloned.1.call-done
  61.6 0.0 copy-start.3
  61.6 9.0 %fusion.20 = (f32[2048]{0:T(1024)S(1)}, f32[64,2048]{1,0:T(8,128)S(1)}, f32[64,8,2048]{2,1,0:T(8,128)}) fusion(f32[64,8]{1,0:T(8,128)S(1)} %bitcast.49, f32[2048]{0:T(1024)} %bitcast.53, bf16[64,8,1024]{2,1,0:T(8,128)(2,1)} %all-gather.5.cloned.1.call-done, bf16[1024,2048]{1,0:T(8,128)(2,1)} %param.12), kind=kOutput, calls=%fused_computation.21 | convolution fusion | flops 2152593408 | bytes 9979904 | tf_op jit(solution)/shard_map/blh,hv->blv/dot_general | solution.py:11
  70.6 0.6 broadcast_multiply_fusion.1
  71.9 41.1 %all-gather.7.cloned.1.call-done = bf16[64,48,1024]{2,1,0:T(8,128)(2,1)} async-done(((bf16[4,48,1024]{2,1,0:T(8,128)(2,1)}), bf16[64,48,1024]{2,1,0:T(8,128)(2,1)}) %all-gather.7.cloned.1.call-update) | async-done | bytes 6291472 | tf_op jit(solution)/shard_map/all_gather | solution.py:37
  113.0 0.0 copy-done.3
  113.0 29.7 %fusion = (f32[2048]{0:T(1024)S(1)}, f32[64,2048]{1,0:T(8,128)S(1)}, f32[64,48,2048]{2,1,0:T(8,128)}) fusion(f32[64,48]{1,0:T(8,128)S(1)} %bitcast.45, f32[2048]{0:T(1024)S(1)} %bitcast.54, bf16[64,48,1024]{2,1,0:T(8,128)(2,1)} %all-gather.7.cloned.1.call-done, bf16[1024,2048]{1,0:T(8,128)(2,1)} %param.12), kind=kOutput, calls=%fused_computation.2 | convolution fusion | flops 12916226048 | bytes 36204544 | tf_op jit(solution)/shard_map/blh,hv->blv/dot_general | solution.py:11
  142.7 0.6 broadcast_multiply_fusion
  143.3 0.6 fusion.37
  144.5 60.4 %all-reduce.1 = (f32[64,64]{1,0:T(8,128)S(1)}, f32[]{:T(128)}) all-reduce(f32[64,64]{1,0:T(8,128)S(1)} %fusion.37, f32[]{:T(128)S(6)} %add.84), channel_id=1, replica_groups=mesh['dp'=2,'tp'=16] {'tp'}, use_global_device_ids=true, to_apply=%region_2.0 | all-reduce | flops 4097 | bytes 32776 | tf_op jit(solution)/shard_map/psum | solution.py:49
  204.9 0.1 reduce_max.9
  205.0 0.2 select_reduce_fusion
  205.2 0.6 subtract_reduce_fusion
  205.8 0.7 convolution_add_fusion
  206.5 1.4 convolution_add_fusion.1
  208.0 0.0 copy-done.1
  208.0 7.0 %fusion.22 = bf16[64,8,1024]{2,1,0:T(8,128)(2,1)} fusion(bf16[1024,2048]{1,0:T(8,128)(2,1)} %param.12, f32[64,8,2048]{2,1,0:T(8,128)} %get-tuple-element.29, f32[64,2048]{1,0:T(8,128)} %convolution_add_fusion.1, f32[64,8]{1,0:T(8,128)S(1)} %bitcast.50, f32[2048]{0:T(1024)S(1)} %bitcast.55), kind=kOutput, calls=%fused_computation.25 | convolution fusion | flops 2156396544 | bytes 9971712 | tf_op jit(solution)/shard_map/blv,hv->blh/dot_general | solution.py:23
  215.0 0.0 reduce-scatter.3.cloned.1.call-update
  215.0 0.0 reduce-scatter.5.cloned.1.call-start
  215.0 21.7 %fusion.14 = bf16[64,48,1024]{2,1,0:T(8,128)(2,1)} fusion(bf16[1024,2048]{1,0:T(8,128)(2,1)} %param.12, f32[64,48,2048]{2,1,0:T(8,128)} %get-tuple-element.30, f32[64,2048]{1,0:T(8,128)S(1)} %convolution_add_fusion, f32[64,48]{1,0:T(8,128)S(1)} %bitcast.46, f32[2048]{0:T(1024)S(1)} %bitcast.56), kind=kOutput, calls=%fused_computation.19 | convolution fusion | flops 12938379264 | bytes 36196352 | tf_op jit(solution)/shard_map/blv,hv->blh/dot_general | solution.py:23
  236.7 0.0 reduce-scatter.5.cloned.1.call-update
  236.7 0.0 copy-start
  236.8 0.0 copy-start.2
  236.8 24.5 %fusion.5 = f32[2048,1024,1]{1,0,2:T(8,128)} fusion(bf16[64,48,1024]{2,1,0:T(8,128)(2,1)} %all-gather.7.cloned.1.call-done, f32[64,48,2048]{2,1,0:T(8,128)} %get-tuple-element.30, f32[64,2048]{1,0:T(8,128)S(1)} %convolution_add_fusion, f32[64,48]{1,0:T(8,128)S(1)} %bitcast.47, f32[2048]{0:T(1024)S(1)} %bitcast.57), kind=kOutput, calls=%fused_computation.8 | convolution fusion | flops 12935233536 | bytes 40390656 | tf_op jit(solution)/shard_map/blh,blv->hv/dot_general | solution.py:22
  261.2 0.0 copy-done
  261.2 0.0 copy-done.2
  261.2 7.1 %fusion.19 = bf16[1024,2048]{0,1:T(8,128)(2,1)} fusion(f32[2048,1024,1]{1,0,2:T(8,128)} %fusion.5, bf16[64,8,1024]{2,1,0:T(8,128)(2,1)} %all-gather.5.cloned.1.call-done, f32[64,8,2048]{2,1,0:T(8,128)S(1)} %copy-done, f32[64,2048]{1,0:T(8,128)} %convolution_add_fusion.1, f32[64,8]{1,0:T(8,128)S(1)} %bitcast.51, f32[2048]{0:T(1024)S(1)} %bitcast.58), kind=kOutput, calls=%fused_computation.20 | convolution fusion | flops 2160066560 | bytes 18360320 | tf_op jit(solution)/shard_map/blh,blv->hv/dot_general | solution.py:22
  268.3 6.4 %copy.21 = bf16[1024,2048]{1,0:T(8,128)(2,1)} copy(bf16[1024,2048]{0,1:T(8,128)(2,1)} %fusion.19) | data formatting | bytes 8388608
  276.1 2.9 fusion.35
  279.0 11.8 %fusion.36 = f32[2048]{0:T(1024)S(1)} fusion(f32[64,48]{1,0:T(8,128)S(1)} %bitcast.48, f32[64,48,2048]{2,1,0:T(8,128)} %get-tuple-element.30, f32[2048]{0:T(1024)S(1)} %bitcast.60, f32[64,2048]{1,0:T(8,128)S(1)} %convolution_add_fusion), kind=kLoop, calls=%fused_computation.48 | loop fusion | flops 50329600 | bytes 25718784 | tf_op jit(solution)/shard_map/reduce_sum | solution.py:20
  290.8 0.6 add.93
  291.4 0.0 reduce-scatter.3.cloned.1.call-done
  291.4 67.2 %reduce-scatter.5.cloned.1.call-done = bf16[4,48,1024]{2,1,0:T(8,128)(2,1)} async-done(((bf16[64,48,1024]{2,1,0:T(8,128)(2,1)}), bf16[4,48,1024]{2,1,0:T(8,128)(2,1)}) %reduce-scatter.5.cloned.1.call-update) | async-done | bytes 393232 | tf_op jit(solution)/shard_map/reduce_scatter | solution.py:60
  (4 shorter events, 0.0 us)
Async XLA Ops:
  7.2 54.5 %all-gather.5.cloned.1.call-start = ((), (), s32[]{:S(2)}) async-start(), calls=%async_computation.2 | async-start | bytes 1114112 | tf_op jit(solution)/shard_map/all_gather | solution.py:36
  7.9 105.1 %all-gather.7.cloned.1.call-start = ((), (), s32[]{:S(2)}) async-start(), calls=%async_computation.3 | async-start | bytes 6684672 | tf_op jit(solution)/shard_map/all_gather | solution.py:37
  8.6 282.8 %reduce-scatter.3.cloned.1.call-start = ((), (), s32[]{:S(2)}) async-start(), calls=%async_computation.4 | async-start | bytes 1114112 | tf_op jit(solution)/shard_map/reduce_scatter | solution.py:59
  31.9 176.0 %copy-start.1 = (f32[16,4,8]{2,1,0:T(4,128)}, f32[16,4,8]{2,1,0:T(4,128)S(1)}, u32[]{:S(2)}) copy-start(f32[16,4,8]{2,1,0:T(4,128)S(1)} %convert_element_type.40) | copy-start | bytes 6148
  61.6 51.4 %copy-start.3 = (f32[1,2048]{1,0:T(1,128)S(1)}, f32[1,2048]{1,0:T(1,128)}, u32[]{:S(2)}) copy-start(f32[1,2048]{1,0:T(1,128)} %param.13) | copy-start | bytes 24580
  215.0 143.6 %reduce-scatter.5.cloned.1.call-start = ((), (), s32[]{:S(2)}) async-start(), calls=%async_computation.5 | async-start | bytes 6684672 | tf_op jit(solution)/shard_map/reduce_scatter | solution.py:60
  236.7 24.5 %copy-start = (f32[64,8,2048]{2,1,0:T(8,128)S(1)}, f32[64,8,2048]{2,1,0:T(8,128)}, u32[]{:S(2)}) copy-start(f32[64,8,2048]{2,1,0:T(8,128)} %get-tuple-element.29) | copy-start | bytes 12582916
  236.8 24.5 %copy-start.2 = (f32[16,4,8]{2,1,0:T(4,128)S(1)}, f32[16,4,8]{2,1,0:T(4,128)}, u32[]{:S(2)}) copy-start(f32[16,4,8]{2,1,0:T(4,128)} %copy-done.1) | copy-start | bytes 6148
Sparse Core Ops, SparseCore 0:
  10.1 40.5 all-gather.4
  53.0 59.9 all-gather.6
  215.1 54.6 reduce-scatter.2
  274.2 84.3 reduce-scatter.4
where the time goes:
time: 367 us; the launch traced here: 366 us
  blocking collectives  111 us (30%)
  waiting for transfers between devices  110 us (30%)
  matrix products  102 us (28%)
  between operations  18.2 us (5%)
  other arithmetic  17.5 us (5%)
  local copies, waits for them, and re-layouts  8.54 us (2%)
    reduce_scatter x1, waiting for transfers between devices, device_step(): grad_doc = lax.psum_scatter(hidden_d, 'tp', scatter_dimension=0, tiled=True)  67.2 us
    psum x1, blocking collectives, device_step(): scores, reg_total = lax.psum((score_part, reg_part), 'tp')  60.4 us
    all_gather x1, waiting for transfers between devices, device_step(): hid_d = lax.all_gather(doc_hidden, 'tp', axis=0, tiled=True)  41.1 us
    dot_general x2, matrix products, head_forward(): jnp.einsum('blh,hv->blv', hidden, head_weight, preferred_element_type=jnp...  38.6 us
    dot_general x2, matrix products, head_backward(): jnp.einsum('blh,blv->hv', hidden, grad_low, preferred_element_type=jnp.fl...  31.6 us
    dot_general x2, matrix products, head_backward(): jnp.einsum('blv,hv->blh', grad_low, head_weight, preferred_element_type=j...  28.7 us
    all_gather x1, blocking collectives, device_step(): keep_q = lax.all_gather(query_mask, 'tp', axis=0, tiled=True)  23.2 us
    all_gather x1, blocking collectives, device_step(): keep_d = lax.all_gather(doc_mask, 'tp', axis=0, tiled=True)  17.5 us
  transfers between devices with their start and end apart: 4, of which 2 were waited for; matrix products, arithmetic and copies ran while one was open for 24% of the time, Pallas kernels for 0%

commit v1 on v0

v1 whole, which is shorter than its diff:
```python
import functools
import math
import jax
import jax.numpy as jnp
from jax import lax
from jax.experimental import pallas as pl
from jax.experimental.pallas import tpu as pltpu
from jax.sharding import PartitionSpec as P

HIGHEST = lax.Precision.HIGHEST
F32 = jnp.float32
BF16 = jnp.bfloat16
TILE = 256
ROWS = 4
NDEV = 16
NT_DIMS = (((1,), (1,)), ((), ()))
TN_DIMS = (((0,), (0,)), ((), ()))

END_AT = (3, 4, 6, 8, 9, 11, 13, 15)
MID_AT = (5, 6, 8, 9, 10, 11, 13, 15)


def kernel(d_len, q_len, lam_q, lam_d,
           xd, xq, md, mq, pos, w, b,
           loss, dw, db, dhd, dhq,
           hid_d, hid_q, meta, wv, hid_t, gate_d, gate_q, rep_d, rep_q, grad_d, grad_q,
           low, part, part_q, in_y, in_l, in_r, in_qz, in_qy, acc, pos_s, s_a, s_b,
           load_sem, meta_ss, meta_rs, qy_ss, qy_rs, qz_ss, qz_rs, qs_ss, qs_rs,
           dl_ss, dr_ss, dz_rs, dy_ss, dy_rs, ds_ss, ds_rs,
           sa_ss, sa_rs, sb_ss, sb_rs,
           bs_ss, bs_rs, by_ss, by_rs, bl_ss, br_ss, bl_rs, br_rs,
           cs_ss, cs_rs, cz_ss, cz_rs, cy_ss, cy_rs):
    n_pair = NDEV // 2
    rd, rq = ROWS * d_len, ROWS * q_len
    half = rd // 2
    hidden = wv.shape[0]
    tiles = wv.shape[1] // TILE
    n_q, n_d = NDEV * ROWS, NDEV * ROWS
    all_d = NDEV * rd
    me = lax.axis_index('tp')
    z, y, c = me // 4, (me // 2) % 2, me % 2
    far = z // 2
    mid = z * (1 - far) + (3 - z) * far
    sib = me + 1 - 2 * c
    over_y = me + 2 - 4 * y
    left, right = me - 4, me + 4

    def order(k):
        o = (k // 2) * k + (1 - k // 2) * ((k + mid) % 2)
        return o * (1 - far) + (3 - o) * far

    def remote(src, dst, ss, rs, dev):
        return pltpu.make_async_remote_copy(
            src_ref=src, dst_ref=dst, send_sem=ss, recv_sem=rs,
            device_id={'tp': dev}, device_id_type=pl.DeviceIdType.MESH)

    def got(dst, rs):
        remote(dst, dst, rs, rs, sib).wait_recv()

    def sent(src, ss):
        remote(src, src, ss, ss, sib).wait_send()

    load_d = pltpu.make_async_copy(xd, hid_d.at[me], load_sem.at[0])
    load_q = pltpu.make_async_copy(xq, hid_q.at[me // 2, c], load_sem.at[1])
    load_w = pltpu.make_async_copy(w, wv, load_sem.at[2])
    load_d.start()
    load_q.start()
    load_w.start()
    barrier = pltpu.get_barrier_semaphore()
    for j in range(1, NDEV):
        pl.semaphore_signal(barrier, inc=1, device_id={'tp': (me + j) % NDEV},
                            device_id_type=pl.DeviceIdType.MESH)
    row16 = lax.broadcasted_iota(jnp.int32, (16, TILE), 0)
    own_meta = jnp.zeros((16, TILE), F32)
    for r in range(ROWS):
        len_d = jnp.sum(md[r:r + 1, :].astype(F32), axis=1, keepdims=True)
        len_q = jnp.sum(mq[r:r + 1, :].astype(F32), axis=1, keepdims=True)
        own_meta = jnp.where(row16 == r, len_d, own_meta)
        own_meta = jnp.where(row16 == ROWS + r, len_q, own_meta)
        own_meta = jnp.where(row16 == 2 * ROWS + r, pos[r].astype(F32), own_meta)
    meta[me] = own_meta.astype(BF16)
    load_d.wait()
    load_q.wait()
    pl.semaphore_wait(barrier, NDEV - 1)

    def doc_half(shard, h):
        return hid_d.at[shard, pl.ds(h * half, half)]

    def pass_on(zs, h):
        ref = doc_half(4 * zs + 2 * y + c, h)
        remote(ref, ref, dy_ss.at[zs, h], dy_rs.at[zs, h], over_y).start()

        @pl.when(jnp.logical_and(zs >= z, z > 0))
        def _():
            remote(ref, ref, dl_ss.at[zs, h], dz_rs.at[zs, h], left).start()

        @pl.when(jnp.logical_and(zs <= z, z < 3))
        def _():
            remote(ref, ref, dr_ss.at[zs, h], dz_rs.at[zs, h], right).start()

        remote(ref, ref, ds_ss.at[2 * zs + y, h], ds_rs.at[2 * zs + y, h], sib).start()

    def arrive_line(zs):
        for h in range(2):
            got(doc_half(4 * zs + 2 * y + c, h), dz_rs.at[zs, h])
            pass_on(zs, h)

    def arrive_over(zs):
        p = 2 * zs + 1 - y
        for h in range(2):
            ref = doc_half(2 * p + c, h)
            got(ref, dy_rs.at[zs, h])
            remote(ref, ref, ds_ss.at[p, h], ds_rs.at[p, h], sib).start()

    def query_out(yy):
        ref = hid_q.at[2 * z + yy, c]
        for j in range(1, 4):
            remote(ref, ref, qz_ss.at[yy, j], qz_rs.at[z, yy], (me + 4 * j) % NDEV).start()

    for j in range(1, NDEV):
        remote(meta.at[me], meta.at[me], meta_ss.at[j], meta_rs.at[me], (me + j) % NDEV).start()
    own_q = hid_q.at[me // 2, c]
    pass_on(z, 0)
    remote(own_q, own_q, qy_ss.at[0], qy_rs.at[0], over_y).start()
    pass_on(z, 1)
    query_out(y)

    @pl.loop(1, NDEV)
    def _(j):
        src = (me + j) % NDEV
        got(meta.at[src], meta_rs.at[src])

    load_w.wait()

    def gated(logits, keep):
        on = jnp.logical_and(logits > 0.0, keep)
        held = jnp.where(on, logits, 0.0)
        up = 1.0 + held
        inv = 1.0 / up
        act = jnp.log(up) + (held - (up - 1.0)) * inv
        return act, jnp.where(on, inv, 0.0)

    place_d = lax.broadcasted_iota(jnp.int32, (d_len, TILE), 0).astype(F32)
    place_q = lax.broadcasted_iota(jnp.int32, (q_len, TILE), 0).astype(F32)

    def tile(n):
        return pl.ds(pl.multiple_of(n * TILE, TILE), TILE)

    def docs_forward(p):
        info = meta[pl.ds(2 * p, 2)].astype(F32)

        @pl.loop(0, tiles)
        def _(n):
            cols = tile(n)
            x = hid_d[pl.ds(2 * p, 2)].reshape(2 * rd, hidden)
            logits = jnp.dot(x, wv[:, cols], preferred_element_type=F32) + b[:, cols]
            for d in range(2 * ROWS):
                keep = place_d < info[d // ROWS, d % ROWS:d % ROWS + 1, :]
                act, gate = gated(logits[d_len * d:d_len * (d + 1)], keep)
                gate_d[pl.ds(p * 2 * rd + d_len * d, d_len), cols] = gate
                rep_d[pl.ds(p * 2 * ROWS + d, 1), cols] = jnp.sum(act, axis=0, keepdims=True)

        @pl.loop(0, hidden // 128)
        def _(t):
            lanes = pl.ds(pl.multiple_of(t * 128, 128), 128)
            block = hid_d[pl.ds(2 * p, 2), :, lanes].reshape(2 * rd, 128)
            hid_t[lanes, pl.ds(pl.multiple_of(p * 2 * rd, 128), 2 * rd)] = block.T

    def queries_forward():
        @pl.loop(0, tiles)
        def _(n):
            cols = tile(n)
            x = hid_q[...].reshape(NDEV * rq, hidden)
            logits = jnp.dot(x, wv[:, cols], preferred_element_type=F32) + b[:, cols]
            for i in range(NDEV):
                info = meta[i].astype(F32)
                for r in range(ROWS):
                    q = ROWS * i + r
                    keep = place_q < info[ROWS + r:ROWS + r + 1, :]
                    act, gate = gated(logits[q_len * q:q_len * (q + 1)], keep)
                    gate_q[q_len * q:q_len * (q + 1), cols] = gate
                    rep_q[q:q + 1, cols] = jnp.sum(act, axis=0, keepdims=True)

        @pl.loop(0, hidden // 128)
        def _(t):
            lanes = pl.ds(pl.multiple_of(t * 128, 128), 128)
            block = hid_q[:, :, :, lanes].reshape(NDEV * rq, 128)
            hid_t[lanes, all_d:all_d + NDEV * rq] = block.T

    def queries_pass():
        got(hid_q.at[2 * z + 1 - y, c], qy_rs.at[0])
        query_out(1 - y)

    def queries_share():
        for j in range(1, 4):
            zs = (z + j) % 4
            for yy in range(2):
                got(hid_q.at[2 * zs + yy, c], qz_rs.at[zs, yy])
        remote(hid_q.at[:, c], hid_q.at[:, c], qs_ss.at[0], qs_rs.at[0], sib).start()

    @pl.loop(0, 8)
    def _(u):
        k, other = u // 2, u % 2

        @pl.when(other == 1)
        def _():
            @pl.when(mid == 0)
            def _():
                @pl.when(k < 3)
                def _():
                    arrive_line(order(k + 1))

            @pl.when(mid == 1)
            def _():
                @pl.when(k == 0)
                def _():
                    queries_pass()
                    arrive_line(order(1))
                    arrive_line(order(2))

                @pl.when(k == 1)
                def _():
                    arrive_line(order(3))

            @pl.when(jnp.logical_and(mid == 0, k == 0))
            def _():
                queries_pass()

            arrive_over(order(k))

            @pl.when(k == 1)
            def _():
                queries_share()

        zs = order(k)
        p = 2 * zs + y + other * (1 - 2 * y)
        for h in range(2):
            got(doc_half(2 * p + 1 - c, h), ds_rs.at[p, h])
        docs_forward(p)

        @pl.when(u == 4)
        def _():
            got(hid_q.at[:, 1 - c], qs_rs.at[0])
            queries_forward()

    for j in range(1, NDEV):
        sent(meta.at[me], meta_ss.at[j])
    sent(own_q, qy_ss.at[0])
    for yy in range(2):
        for j in range(1, 4):
            sent(own_q, qz_ss.at[yy, j])
    sent(hid_q.at[:, c], qs_ss.at[0])
    for h in range(2):
        for zs in range(4):
            ref = doc_half(me, h)
            sent(ref, dy_ss.at[zs, h])

            @pl.when(jnp.logical_and(zs >= z, z > 0))
            def _():
                sent(ref, dl_ss.at[zs, h])

            @pl.when(jnp.logical_and(zs <= z, z < 3))
            def _():
                sent(ref, dr_ss.at[zs, h])
        for p in range(n_pair):
            sent(ref, ds_ss.at[p, h])

    mean_q = jnp.mean(rep_q[...], axis=0, keepdims=True)
    mean_d = jnp.mean(rep_d[...], axis=0, keepdims=True)
    reg = (lam_q * jnp.sum(mean_q * mean_q, axis=1, keepdims=True)
           + lam_d * jnp.sum(mean_d * mean_d, axis=1, keepdims=True))
    quad = 2 * y + c
    s_a[quad, :, 0:n_d] = lax.dot_general(rep_q[...], rep_d[...], NT_DIMS, precision=HIGHEST,
                                          preferred_element_type=F32)
    s_a[quad, :, n_d:2 * n_d] = jnp.broadcast_to(reg, (n_q, n_d))
    for j in range(1, 4):
        remote(s_a.at[quad], s_a.at[quad], sa_ss.at[j], sa_rs.at[quad], 4 * z + (quad + j) % 4).start()
    for i in range(NDEV):
        info = meta[i].astype(F32)
        pos_s[ROWS * i:ROWS * (i + 1), :] = info[2 * ROWS:3 * ROWS, 0:128]
    for j in range(1, 4):
        src = (quad + j) % 4
        got(s_a.at[src], sa_rs.at[src])
    s_b[z] = s_a[0] + s_a[1] + s_a[2] + s_a[3]
    for j in range(1, 4):
        remote(s_b.at[z], s_b.at[z], sb_ss.at[j], sb_rs.at[z], (me + 4 * j) % NDEV).start()
    for j in range(1, 4):
        src = (z + j) % 4
        got(s_b.at[src], sb_rs.at[src])
    total = s_b[0] + s_b[1] + s_b[2] + s_b[3]
    scores = total[:, 0:n_d]
    top = jnp.max(scores, axis=1, keepdims=True)
    log_norm = top + jnp.log(jnp.sum(jnp.exp(scores - top), axis=1, keepdims=True))
    lane = lax.broadcasted_iota(jnp.int32, (n_q, n_d), 1).astype(F32)
    target = (pos_s[:, 0:n_d] == lane).astype(F32)
    picked = jnp.sum(target * scores, axis=1, keepdims=True)
    cross = jnp.sum(log_norm - picked, axis=0, keepdims=True) / n_q
    loss[...] = cross + total[0:1, n_d:n_d + 1]
    grad_s = (jnp.exp(scores - log_norm) - target) / n_q

    @pl.loop(0, tiles)
    def _(n):
        cols = tile(n)
        rep_qn, rep_dn = rep_q[:, cols], rep_d[:, cols]
        grad_q[:, cols] = lax.dot_general(
            grad_s, rep_dn, (((1,), (0,)), ((), ())), precision=HIGHEST, preferred_element_type=F32
        ) + (2.0 * lam_q / n_q) * jnp.mean(rep_qn, axis=0, keepdims=True)
        grad_d[:, cols] = lax.dot_general(
            grad_s, rep_qn, TN_DIMS, precision=HIGHEST, preferred_element_type=F32
        ) + (2.0 * lam_d / n_d) * jnp.mean(rep_dn, axis=0, keepdims=True)

    db[...] = jnp.zeros_like(db)
    for j in range(1, 4):
        sent(s_a.at[0], sa_ss.at[j])
        sent(s_b.at[0], sb_ss.at[j])

    def pair_of(j):
        zs = order(3 - j // 2)
        other = 1 - j % 2
        return zs, 2 * zs + y + other * (1 - 2 * y)

    def hidden_grad(rows, store):
        @pl.loop(0, hidden // TILE)
        def _(t):
            hrows = tile(t)
            out = jnp.zeros((rows, TILE), F32)
            for n in range(tiles):
                out = out + lax.dot_general(
                    low[n * rows:(n + 1) * rows, :], wv[hrows, n * TILE:(n + 1) * TILE],
                    NT_DIMS, preferred_element_type=F32)
            store(hrows, out.astype(BF16))

    def docs_gate(p):
        rows = 2 * rd

        @pl.loop(0, tiles)
        def _(n):
            cols = tile(n)
            total_b = jnp.zeros((1, TILE), F32)
            for d in range(2 * ROWS):
                gz = grad_d[pl.ds(2 * ROWS * p + d, 1), cols] * gate_d[pl.ds(p * rows + d_len * d, d_len), cols]
                total_b = total_b + jnp.sum(gz, axis=0, keepdims=True)
                low[pl.ds(pl.multiple_of(n * rows + d_len * d, 16), d_len), :] = gz.astype(BF16)
            db[:, cols] += total_b

    def docs_hidden(slot):
        def store(hrows, out):
            part[slot, :, :, hrows] = out.reshape(2, rd, TILE)
        hidden_grad(2 * rd, store)

    def two_queries(q, cols):
        return jnp.concatenate(
            [grad_q[q + i:q + i + 1, cols] * gate_q[q_len * (q + i):q_len * (q + i + 1), cols]
             for i in range(2)], axis=0)

    def queries_back():
        rows = NDEV * rq

        @pl.loop(0, tiles)
        def _(n):
            cols = tile(n)
            total_b = jnp.zeros((1, TILE), F32)
            for q in range(0, n_q, 2):
                gz = two_queries(q, cols)
                total_b = total_b + jnp.sum(gz, axis=0, keepdims=True)
                low[pl.ds(pl.multiple_of(n * rows + q_len * q, 16), 2 * q_len), :] = gz.astype(BF16)
            db[:, cols] += total_b

        def store(hrows, out):
            part_q[:, :, :, hrows] = out.reshape(n_pair, 2, rq, TILE)
        hidden_grad(rows, store)
        remote(part_q.at[:, 1 - c], hid_q.at[:, 1], cs_ss.at[0], cs_rs.at[0], sib).start()

    def queries_chip():
        got(hid_q.at[:, 1], cs_rs.at[0])

        @pl.loop(0, n_pair)
        def _(p):
            hid_q[p, 0] = (part_q[p, c].astype(F32) + hid_q[p, 1].astype(F32)).astype(BF16)
        for j in range(1, 4):
            zs = (z + j) % 4
            remote(hid_q.at[pl.ds(2 * zs, 2), 0], in_qz.at[z], cz_ss.at[j], cz_rs.at[z],
                   (me + 4 * j) % NDEV).start()

    def queries_line():
        for j in range(1, 4):
            src = (z + j) % 4
            got(in_qz.at[src], cz_rs.at[src])
        for yy in range(2):
            p = 2 * z + yy
            s = hid_q[p, 0].astype(F32)
            for j in range(1, 4):
                s = s + in_qz[(z + j) % 4, yy].astype(F32)
            hid_q[p, 0] = s.astype(BF16)
        remote(hid_q.at[2 * z + 1 - y, 0], in_qy, cy_ss.at[0], cy_rs.at[0], over_y).start()

    def queries_end():
        got(in_qy, cy_rs.at[0])
        dhq[...] = (hid_q[2 * z + y, 0].astype(F32) + in_qy[...].astype(F32)).astype(BF16)

    def chip_sum(j):
        zs, p = pair_of(j)
        slot = j % 2
        got(hid_d.at[n_pair + p], bs_rs.at[p])

        @pl.loop(0, rd // 32)
        def _(t):
            r = pl.ds(pl.multiple_of(t * 32, 32), 32)
            hid_d[p, r] = (part[slot, c, r].astype(F32) + hid_d[n_pair + p, r].astype(F32)).astype(BF16)

        @pl.when(j % 2 == 0)
        def _():
            for h in range(2):
                r = pl.ds(h * half, half)
                remote(hid_d.at[p, r], in_y.at[zs, r], by_ss.at[zs, h], by_rs.at[zs, h], over_y).start()

    def line_step(e):
        k, h = 3 - e // 2, e % 2
        d = order(k)
        p = 2 * d + y
        r = pl.ds(h * half, half)
        from_left = jnp.logical_and(z > 0, d >= z)
        from_right = jnp.logical_and(z < 3, d <= z)
        left_slot = jnp.maximum(d - 1, 0)
        right_slot = jnp.minimum(d, 2)
        got(in_y.at[d, r], by_rs.at[d, h])
        acc[...] = hid_d[p, r].astype(F32) + in_y[d, r].astype(F32)

        @pl.when(from_left)
        def _():
            got(in_l.at[left_slot, r], bl_rs.at[d, h])
            acc[...] += in_l[left_slot, r].astype(F32)

        @pl.when(from_right)
        def _():
            got(in_r.at[right_slot, r], br_rs.at[d, h])
            acc[...] += in_r[right_slot, r].astype(F32)

        if k == 0:
            dhd[r] = acc[...].astype(BF16)
        else:
            hid_d[p, r] = acc[...].astype(BF16)

            @pl.when(d < z)
            def _():
                remote(hid_d.at[p, r], in_r.at[jnp.minimum(d, 2), r], bl_ss.at[d, h], br_rs.at[d, h], left).start()

            @pl.when(d > z)
            def _():
                remote(hid_d.at[p, r], in_l.at[jnp.maximum(d - 1, 0), r], br_ss.at[d, h], bl_rs.at[d, h], right).start()

    def weight_grad(n):
        cols = tile(n)

        @pl.loop(0, n_d // 8)
        def _(t):
            for i in range(8):
                d = t * 8 + i
                r = pl.ds(pl.multiple_of(d * d_len, 16), d_len)
                low[r, :] = (grad_d[pl.ds(d, 1), cols] * gate_d[r, cols]).astype(BF16)
        for q in range(0, n_q, 2):
            low[all_d + q_len * q:all_d + q_len * (q + 2), :] = two_queries(q, cols).astype(BF16)
        depth = all_d + NDEV * rq
        step = min(512, hidden)

        @pl.loop(0, hidden // step)
        def _(m):
            r = pl.ds(pl.multiple_of(m * step, step), step)
            dw[r, cols] = jnp.dot(hid_t[r, :], low[0:depth, :], preferred_element_type=F32).astype(BF16)

    @pl.loop(0, 9 + tiles)
    def _(u):
        @pl.when(jnp.logical_and(u < 9, u != 4))
        def _():
            j = u - u // 5
            slot = j % 2
            zs, p = pair_of(j)
            docs_gate(p)

            @pl.when(j >= 1)
            def _():
                chip_sum(j - 1)

            @pl.when(j >= 2)
            def _():
                sent(part.at[0, 0], bs_ss.at[slot])
            docs_hidden(slot)
            remote(part.at[slot, 1 - c], hid_d.at[n_pair + p], bs_ss.at[slot], bs_rs.at[p], sib).start()

        @pl.when(u == 4)
        def _():
            queries_back()

        @pl.when(u == 6)
        def _():
            queries_chip()

        @pl.when(u == 9)
        def _():
            chip_sum(7)
            queries_line()

        @pl.when(u >= 9)
        def _():
            weight_grad(u - 9)

        for e in range(8):
            at = END_AT[e] * (1 - mid) + MID_AT[e] * mid

            @pl.when(u == jnp.minimum(at, 8 + tiles))
            def _():
                line_step(e)

    queries_end()
    for slot in range(2):
        sent(part.at[0, 0], bs_ss.at[slot])
    sent(part_q.at[:, 0], cs_ss.at[0])
    for j in range(1, 4):
        sent(in_qz.at[0], cz_ss.at[j])
    sent(in_qy, cy_ss.at[0])
    for h in range(2):
        for zs in range(4):
            ref = in_y.at[0, pl.ds(0, half)]
            sent(ref, by_ss.at[zs, h])

            @pl.when(zs < z)
            def _():
                sent(ref, bl_ss.at[zs, h])

            @pl.when(zs > z)
            def _():
                sent(ref, br_ss.at[zs, h])


def solution(mesh):
    group_size = mesh.shape['tp']

    def device_step(query_hidden, doc_hidden, query_mask, doc_mask, positives, head_weight, head_bias):
        hidden, cols = head_weight.shape
        vocab_size = cols * group_size
        q_len = query_hidden.shape[1]
        d_len = doc_hidden.shape[1]
        lam_q = math.sqrt(d_len) / (4.0 * math.sqrt(vocab_size) * q_len)
        lam_d = q_len / (4.0 * math.sqrt(vocab_size) * d_len ** 1.5)
        rd, rq = ROWS * d_len, ROWS * q_len
        n_q = NDEV * ROWS
        all_d, all_q = NDEV * rd, NDEV * rq
        tiles = cols // TILE
        vmem = pl.BlockSpec(memory_space=pltpu.VMEM)
        hbm = pl.BlockSpec(memory_space=pl.ANY)
        dma = pltpu.SemaphoreType.DMA
        low_rows = max(tiles * max(all_q, 2 * rd), all_d + all_q)
        out = pl.pallas_call(
            functools.partial(kernel, d_len, q_len, lam_q, lam_d),
            out_shape=[
                jax.ShapeDtypeStruct((1, 1), F32),
                jax.ShapeDtypeStruct((hidden, cols), BF16),
                jax.ShapeDtypeStruct((1, cols), F32),
                jax.ShapeDtypeStruct((rd, hidden), BF16),
                jax.ShapeDtypeStruct((rq, hidden), BF16),
            ],
            in_specs=[hbm, hbm, vmem, vmem, pl.BlockSpec(memory_space=pltpu.SMEM), hbm, vmem],
            out_specs=[vmem] * 5,
            scratch_shapes=[
                pltpu.VMEM((NDEV, rd, hidden), BF16),
                pltpu.VMEM((NDEV // 2, 2, rq, hidden), BF16),
                pltpu.VMEM((NDEV, 16, TILE), BF16),
                pltpu.VMEM((hidden, cols), BF16),
                pltpu.VMEM((hidden, all_d + all_q), BF16),
                pltpu.VMEM((all_d, cols), F32),
                pltpu.VMEM((all_q, cols), F32),
                pltpu.VMEM((n_q, cols), F32),
                pltpu.VMEM((n_q, cols), F32),
                pltpu.VMEM((n_q, cols), F32),
                pltpu.VMEM((n_q, cols), F32),
                pltpu.VMEM((low_rows, TILE), BF16),
                pltpu.VMEM((2, 2, rd, hidden), BF16),
                pltpu.VMEM((NDEV // 2, 2, rq, hidden), BF16),
                pltpu.VMEM((4, rd, hidden), BF16),
                pltpu.VMEM((3, rd, hidden), BF16),
                pltpu.VMEM((3, rd, hidden), BF16),
                pltpu.VMEM((4, 2, rq, hidden), BF16),
                pltpu.VMEM((rq, hidden), BF16),
                pltpu.VMEM((rd // 2, hidden), F32),
                pltpu.VMEM((n_q, 128), F32),
                pltpu.VMEM((4, n_q, 128), F32),
                pltpu.VMEM((4, n_q, 128), F32),
                dma((3,)), dma((NDEV,)), dma((NDEV,)), dma((1,)), dma((1,)), dma((2, 4)), dma((4, 2)), dma((1,)), dma((1,)),
                dma((4, 2)), dma((4, 2)), dma((4, 2)), dma((4, 2)), dma((4, 2)), dma((8, 2)), dma((8, 2)),
                dma((4,)), dma((4,)), dma((4,)), dma((4,)),
                dma((2,)), dma((8,)), dma((4, 2)), dma((4, 2)), dma((4, 2)), dma((4, 2)), dma((4, 2)), dma((4, 2)),
                dma((1,)), dma((1,)), dma((4,)), dma((4,)), dma((1,)), dma((1,)),
            ],
            compiler_params=pltpu.CompilerParams(
                collective_id=0, has_side_effects=True, vmem_limit_bytes=67043328),
        )(doc_hidden.reshape(rd, hidden), query_hidden.reshape(rq, hidden), doc_mask, query_mask, positives,
          head_weight, head_bias)
        total_loss, grad_weight, grad_bias, grad_doc, grad_query = out
        return (total_loss.reshape(1), grad_weight, grad_bias,
                grad_query.reshape(query_hidden.shape), grad_doc.reshape(doc_hidden.shape))

    batch_rows = P(('dp', 'tp'), None, None)
    batch_masks = P(('dp', 'tp'), None)
    return jax.shard_map(device_step, mesh=mesh, in_specs=(batch_rows, batch_rows, batch_masks, batch_masks, P(('dp', 'tp')), P(None, 'tp'), P(None, 'tp')), out_specs=(P('dp'), P('dp', 'tp'), P('dp', 'tp'), batch_rows, batch_rows), check_vma=False)
```

time: 367 us -> 162 us (0.44)
  Pallas kernels: 0 us -> 152 us
  blocking collectives: 111 us -> 0 us
  waiting for transfers between devices: 110 us -> 0 us
  matrix products: 102 us -> 0 us
  other arithmetic: 17.5 us -> 0 us
  between operations: 18.2 us -> 2.43 us
    pallas_call x0 -> x1, Pallas kernels: none -> 152 us  [device_step(): pl.pallas_call(functools.partial(kernel, d_len, q_len, lam_q, lam_d), out...]
    dot_general x9 -> x0, matrix products: 102 us -> none  [the longest x2 38.6 us: head_forward(): jnp.einsum('blh,hv->blv', hidden, head_weight, preferred_element_type=jnp...]
    reduce_scatter x2 -> x0, waiting for transfers between devices: 67.2 us -> none  [the longest x1 67.2 us: device_step(): grad_doc = lax.psum_scatter(hidden_d, 'tp', scatter_dimension=0, tiled=True)]
    psum x1 -> x0, blocking collectives: 60.4 us -> none  [device_step(): scores, reg_total = lax.psum((score_part, reg_part), 'tp')]
    all_gather x2 -> x0, waiting for transfers between devices: 41.1 us -> none  [the longest x1 41.1 us: device_step(): hid_d = lax.all_gather(doc_hidden, 'tp', axis=0, tiled=True)]
    all_gather x2 -> x0, blocking collectives: 40.8 us -> none  [the longest x1 23.2 us: device_step(): keep_q = lax.all_gather(query_mask, 'tp', axis=0, tiled=True)]
    reduce_sum x4 -> x0, other arithmetic: 15.5 us -> none  [the longest x2 14.7 us: head_backward(): bias_part = jnp.sum(grad_logits, axis=(0, 1))]
    unnamed x1 -> x0, blocking collectives: 9.37 us -> none
  transfers between devices with their start and end apart: 4 -> 0, of which waited for: 2 -> 0; matrix products, arithmetic and copies ran while one was open for 24% -> 0% of each run, Pallas kernels for 0% -> 0%
where the time goes in v1:
time: 162 us; the launch traced here: 161 us
  Pallas kernels  152 us (94%)
  local copies, waits for them, and re-layouts  6.83 us (4%)
  between operations  2.43 us (2%)
    pallas_call x1, Pallas kernels, device_step(): pl.pallas_call(functools.partial(kernel, d_len, q_len, lam_q, lam_d), out...  152 us
    unnamed x10, local copies, waits for them, and re-layouts  6.83 us

profile of v1, /device:TPU:0, one launch (start us, length us, event | category | flops | bytes accessed | tf_op | source)
XLA Modules:
  0.0 161.2 jit_solution(7613818118784490345)
XLA Ops:
  0.6 151.9 %shard_map.110 = (f32[1,1]{1,0:T(1,128)}, bf16[1024,2048]{1,0:T(8,128)(2,1)}, f32[1,2048]{1,0:T(1,128)}, bf16[192,1024]{1,0:T(8,128)(2,1)}, bf16[32,1024]{1,0:T(8,128)(2,1)}) custom-call(bf16[192,1024]{1,0:T(8,128)(2,1)} %bitcast.5, bf16[32,1024]{1,0:T(8,128)(2,1)} %bitcast.7, s32[4,48]{1,0:T(4,128)} %md.1, s32[4,8]{1,0:T(4,128)} %mq.1, s32[4]{0:T(128)} %pos.1, ...), custom_call_target="tpu_custom_call" | custom-call | tf_op jit(solution)/shard_map/pallas_call | solution.py:553
  153.2 0.0 copy-start.2
  153.2 0.0 copy-start.1
  153.2 0.0 copy-start
  153.2 4.8 %copy.18 = bf16[1024,2048]{1,0:T(8,128)(2,1)} copy(bf16[1024,2048]{1,0:T(8,128)(2,1)} %get-tuple-element.21) | data formatting | bytes 8388608
  158.1 0.0 copy-done.2
  158.1 0.6 copy.19
  158.7 0.0 copy-done.1
  158.7 0.6 copy.20
  159.3 0.0 copy-done
  159.3 0.7 copy.21
Async XLA Ops:
  153.2 4.9 %copy-start.2 = (f32[1,2048]{1,0:T(1,128)S(1)}, f32[1,2048]{1,0:T(1,128)}, u32[]{:S(2)}) copy-start(f32[1,2048]{1,0:T(1,128)} %get-tuple-element.22) | copy-start | bytes 24580
  153.2 5.5 %copy-start.1 = (bf16[32,1024]{1,0:T(8,128)(2,1)S(1)}, bf16[32,1024]{1,0:T(8,128)(2,1)}, u32[]{:S(2)}) copy-start(bf16[32,1024]{1,0:T(8,128)(2,1)} %get-tuple-element.13) | copy-start | bytes 196612
  153.2 6.1 %copy-start = (bf16[192,1024]{1,0:T(8,128)(2,1)S(1)}, bf16[192,1024]{1,0:T(8,128)(2,1)}, u32[]{:S(2)}) copy-start(bf16[192,1024]{1,0:T(8,128)(2,1)} %get-tuple-element.14) | copy-start | bytes 1179652

commit v2 on v1

v2 whole, which is shorter than its diff:
```python
import functools
import math
import jax
import jax.numpy as jnp
from jax import lax
from jax.experimental import pallas as pl
from jax.experimental.pallas import tpu as pltpu
from jax.sharding import PartitionSpec as P

HIGHEST = lax.Precision.HIGHEST
F32 = jnp.float32
BF16 = jnp.bfloat16
TILE = 256
ROWS = 4
NDEV = 16
N_Z, SIDES = 4, 2
PAIR = SIDES * ROWS
OTHERS = (1, 2, 3)
DOWN = dict(axis=0, keepdims=True)
ACROSS = dict(axis=1, keepdims=True)
NT_DIMS = (((1,), (1,)), ((), ()))
TN_DIMS = (((0,), (0,)), ((), ()))

END_AT = (4, 5, 6, 8, 9, 11, 14, 16)
MID_AT = (8, 9, 11, 13, 11, 13, 15, 16)


def kernel(d_len, q_len, lam_q, lam_d,
           xd, xq, md, mq, pos, w, b,
           loss, dw_out, db, dhd, dhq,
           hid_d, hid_q, meta, meta_chip, wv, dw, hid_t, gate_d, gate_q, rep_d, rep_q,
           low, part, part_q, in_y, in_l, in_r, in_qz, in_qy, z_even, z_odd, pos_s, s_a, s_b,
           load_sem, out_sem, meta_ss, meta_rs, qy_ss, qy_rs, qz_ss, qz_rs, qs_ss, qs_rs,
           dl_ss, dr_ss, dz_rs, dy_ss, dy_rs, ds_ss, ds_rs,
           sa_ss, sa_rs, sb_ss, sb_rs,
           bs_ss, bs_rs, by_ss, by_rs, bl_ss, br_ss, bl_rs, br_rs,
           cs_ss, cs_rs, cz_ss, cz_rs, cy_ss, cy_rs):
    n_pair = NDEV // 2
    rd, rq = ROWS * d_len, ROWS * q_len
    half = rd // 2
    hidden = wv.shape[0]
    tiles = wv.shape[1] // TILE
    n_q, n_d = NDEV * ROWS, NDEV * ROWS
    all_d = NDEV * rd
    me = lax.axis_index('tp')
    z, y, c = me // 4, (me // 2) % 2, me % 2
    far = z // 2
    mid = z * (1 - far) + (3 - z) * far
    sib = me + 1 - 2 * c
    over_y = me + 2 - 4 * y
    left, right = me - 4, me + 4

    pair_rows = SIDES * rd
    rounds = N_Z * ROWS

    def spot(zs, yy):
        return SIDES * zs + yy

    def order(k):
        o = (k // 2) * k + (1 - k // 2) * ((k + mid) % 2)
        return o * (1 - far) + (3 - o) * far

    def remote(src, dst, ss, rs, dev):
        return pltpu.make_async_remote_copy(
            src_ref=src, dst_ref=dst, send_sem=ss, recv_sem=rs,
            device_id={'tp': dev}, device_id_type=pl.DeviceIdType.MESH)

    def got(dst, rs):
        remote(dst, dst, rs, rs, sib).wait_recv()

    def sent(src, ss):
        remote(src, src, ss, ss, sib).wait_send()

    def tile(n):
        return pl.ds(pl.multiple_of(n * TILE, TILE), TILE)

    fold = hidden // TILE

    def w_block(n, first, size):
        return pl.ds((n % fold) * TILE, TILE), pl.ds(pl.multiple_of((n // fold) * hidden + first, TILE), size)

    def transpose_weight():
        @pl.loop(0, hidden // TILE)
        def _(t):
            for n in range(tiles):
                r, l = w_block(n, t * TILE, TILE)
                dw[r, l] = wv[tile(t), n * TILE:(n + 1) * TILE].T

    load_d = pltpu.make_async_copy(xd, hid_d.at[me], load_sem.at[0])
    load_q = pltpu.make_async_copy(xq, hid_q.at[me // 2, c], load_sem.at[1])
    load_w = pltpu.make_async_copy(w, wv, load_sem.at[2])
    load_d.start()
    load_q.start()
    load_w.start()
    barrier = pltpu.get_barrier_semaphore()
    line = [(me + 4 * j) % NDEV for j in OTHERS]
    quad = 2 * y + c
    plane = [4 * z + (quad + j) % 4 for j in OTHERS]
    for dev in line + plane:
        pl.semaphore_signal(barrier, inc=1, device_id={'tp': dev}, device_id_type=pl.DeviceIdType.MESH)
    row16 = lax.broadcasted_iota(jnp.int32, (16, TILE), 0)
    own_meta = jnp.zeros((16, TILE), F32)
    for r in range(ROWS):
        len_d = jnp.sum(md[r:r + 1, :].astype(F32), **ACROSS)
        len_q = jnp.sum(mq[r:r + 1, :].astype(F32), **ACROSS)
        own_meta = jnp.where(row16 == r, len_d, own_meta)
        own_meta = jnp.where(row16 == ROWS + r, len_q, own_meta)
        own_meta = jnp.where(row16 == PAIR + r, pos[r].astype(F32), own_meta)
    own_meta = own_meta.astype(BF16)
    meta[z, y, c] = own_meta
    meta_chip[c] = own_meta
    load_w.wait()
    transpose_weight()
    load_d.wait()
    load_q.wait()
    pl.semaphore_wait(barrier, 6)

    def doc(shard, q):
        return hid_d.at[shard, pl.ds(pl.multiple_of(q * d_len, 16), d_len)]

    def to_sib(p, q):
        ref = doc(SIDES * p + c, q)
        remote(ref, ref, ds_ss.at[p, q], ds_rs.at[p, q], sib).start()

    def pass_on(zs, q):
        ref = doc(SIDES * spot(zs, y) + c, q)

        @pl.when(jnp.logical_and(zs >= z, z > 0))
        def _():
            remote(ref, ref, dl_ss.at[zs, q], dz_rs.at[zs, q], left).start()

        @pl.when(jnp.logical_and(zs <= z, z < 3))
        def _():
            remote(ref, ref, dr_ss.at[zs, q], dz_rs.at[zs, q], right).start()

        remote(ref, ref, dy_ss.at[zs, q], dy_rs.at[zs, q], over_y).start()
        to_sib(spot(zs, y), q)

    def arrive_line(k, q):
        zs = order(k)
        got(doc(SIDES * spot(zs, y) + c, q), dz_rs.at[zs, q])
        pass_on(zs, q)

    def arrive_over(k, q):
        zs = order(k)
        p = spot(zs, 1 - y)
        got(doc(SIDES * p + c, q), dy_rs.at[zs, q])
        to_sib(p, q)

    def query_out(yy):
        ref = hid_q.at[spot(z, yy), c]
        for j in OTHERS:
            remote(ref, ref, qz_ss.at[yy, j], qz_rs.at[z, yy], (me + 4 * j) % NDEV).start()

    def meta_over():
        for j in OTHERS:
            zs = (z + j) % N_Z
            got(meta.at[zs, y, c], meta_rs.at[zs])
        remote(meta.at[:, y, c], meta.at[:, y, c], meta_ss.at[4], meta_rs.at[4], over_y).start()

    def meta_share():
        got(meta.at[:, 1 - y, c], meta_rs.at[4])
        remote(meta.at[:, :, c], meta.at[:, :, c], meta_ss.at[5], meta_rs.at[5], sib).start()

    own_q = hid_q.at[me // 2, c]
    remote(meta_chip.at[c], meta_chip.at[c], meta_ss.at[0], meta_rs.at[6], sib).start()
    for j in OTHERS:
        remote(meta.at[z, y, c], meta.at[z, y, c], meta_ss.at[j], meta_rs.at[z], line[j - 1]).start()
    pass_on(z, 0)
    for q in range(1, ROWS):
        pass_on(z, q)
    remote(own_q, own_q, qy_ss.at[0], qy_rs.at[0], over_y).start()

    @pl.when(mid == 0)
    def _():
        query_out(y)

    def arrivals(e):
        g, q = e // ROWS, e % ROWS

        @pl.when(mid == 0)
        def _():
            @pl.when(g < 3)
            def _():
                arrive_line(g + 1, q)

        @pl.when(mid == 1)
        def _():
            @pl.when(g == 0)
            def _():
                arrive_line(1, q)
                arrive_line(2, q)

            @pl.when(g == 1)
            def _():
                arrive_line(3, q)

        arrive_over(g, q)

        @pl.when(e == PAIR - 1)
        def _():
            @pl.when(mid == 1)
            def _():
                query_out(y)
            got(hid_q.at[spot(z, 1 - y), c], qy_rs.at[0])
            query_out(1 - y)

    def pump(v):
        last = jnp.minimum(v + 3, rounds) - 2 * (1 // (v + 1))

        @pl.loop(jnp.minimum(v + 2 * jnp.minimum(v // 2, 1), rounds), last)
        def _(e):
            arrivals(e)

        pl.when(v == 0)(meta_over)
        pl.when(v == 1)(meta_share)

    got(meta_chip.at[1 - c], meta_rs.at[6])

    def gated(logits, cap):
        held = jnp.maximum(jnp.minimum(logits, cap), 0.0)
        up = 1.0 + held
        inv = 1.0 / up
        act = jnp.log(up) + (held - (up - 1.0)) * inv
        return act, jnp.where(held > 0.0, inv, 0.0)

    place_d = lax.broadcasted_iota(jnp.int32, (d_len, 128), 0).astype(F32)
    place_q = lax.broadcasted_iota(jnp.int32, (q_len, 128), 0).astype(F32)

    def cap_of(place, length):
        cap = jnp.where(place < length, jnp.finfo(F32).max, 0.0)
        return jnp.concatenate([cap, cap], axis=1)

    def forward(rows, load, finish, transpose, beside):
        def product(n, z_ref):
            z_ref[0:rows, :] = jnp.dot(load(), wv[:, tile(n)], preferred_element_type=F32)

        product(0, z_even)

        @pl.loop(0, tiles // 2)
        def _(i):
            n = 2 * i
            product(n + 1, z_odd)
            finish(n, z_even)
            transpose(n)
            product(jnp.minimum(n + 2, tiles - 1), z_even)
            finish(n + 1, z_odd)
            transpose(n + 1)
            beside(i)

    lane_step = hidden // tiles

    def docs_forward(p, beside):
        info = meta_chip[...].astype(F32)

        def load():
            return hid_d[pl.ds(SIDES * p, SIDES)].reshape(pair_rows, hidden)

        def finish(n, z_ref):
            cols = tile(n)
            bias = b[:, cols]
            for d in range(PAIR):
                cap = cap_of(place_d, info[d // ROWS, d % ROWS:d % ROWS + 1, 0:128])
                act, gate = gated(z_ref[d_len * d:d_len * (d + 1), :] + bias, cap)
                gate_d[pl.ds(p * pair_rows + d_len * d, d_len), cols] = gate
                rep_d[pl.ds(p * PAIR + d, 1), cols] = jnp.sum(act, **DOWN)

        def transpose(n):
            lanes = pl.ds(pl.multiple_of(n * lane_step, lane_step), lane_step)
            block = hid_d[pl.ds(SIDES * p, SIDES), :, lanes].reshape(pair_rows, lane_step)
            hid_t[lanes, pl.ds(pl.multiple_of(p * pair_rows, 128), pair_rows)] = block.T

        forward(pair_rows, load, finish, transpose, beside)

    def queries_forward():
        def load():
            return hid_q[...].reshape(NDEV * rq, hidden)

        def finish(n, z_ref):
            cols = tile(n)
            bias = b[:, cols]
            for i in range(NDEV):
                info = meta[i // N_Z, (i // SIDES) % SIDES, i % SIDES].astype(F32)
                for r in range(ROWS):
                    q = ROWS * i + r
                    cap = cap_of(place_q, info[ROWS + r:ROWS + r + 1, 0:128])
                    act, gate = gated(z_ref[q_len * q:q_len * (q + 1), :] + bias, cap)
                    gate_q[q_len * q:q_len * (q + 1), cols] = gate
                    rep_q[q:q + 1, cols] = jnp.sum(act, **DOWN)

        def transpose(n):
            lanes = pl.ds(pl.multiple_of(n * lane_step, lane_step), lane_step)
            block = hid_q[:, :, :, lanes].reshape(NDEV * rq, lane_step)
            hid_t[lanes, all_d:all_d + NDEV * rq] = block.T

        forward(NDEV * rq, load, finish, transpose, lambda i: None)

    def queries_share():
        for j in OTHERS:
            zs = (z + j) % N_Z
            for yy in range(SIDES):
                got(hid_q.at[spot(zs, yy), c], qz_rs.at[zs, yy])
        remote(hid_q.at[:, c], hid_q.at[:, c], qs_ss.at[0], qs_rs.at[0], sib).start()

    every = max(tiles // 4, 1)

    @pl.loop(0, n_pair)
    def _(u):
        end, odd, some = u // 7, u % 2, (u + 6) // 7
        other = end + (1 - end) * (1 - odd) * some
        k = end * 3 + (1 - end) * (odd * ((u + 1) // 2) + (1 - odd) * some * (u // 2 - 1))
        p = 2 * order(k) + y + other * (1 - 2 * y)

        @pl.when(u == 7)
        def _():
            queries_share()

        for q in range(ROWS):
            got(doc(SIDES * p + 1 - c, q), ds_rs.at[p, q])

        def beside(i):
            @pl.when(i % every == every - 1)
            def _():
                pump(2 * u + i // every)

        @pl.when(u == 1)
        def _():
            got(meta.at[:, :, 1 - c], meta_rs.at[5])

        @pl.when(u > 0)
        def _():
            meta_chip[...] = meta[p // 2, p % 2]
        docs_forward(p, beside)

        @pl.when(u == 0)
        def _():
            sent(meta_chip.at[c], meta_ss.at[0])

    got(hid_q.at[:, 1 - c], qs_rs.at[0])
    queries_forward()

    for j in OTHERS:
        sent(meta.at[z, y, c], meta_ss.at[j])
    sent(meta.at[:, y, c], meta_ss.at[4])
    sent(meta.at[:, :, c], meta_ss.at[5])
    sent(own_q, qy_ss.at[0])
    for yy in range(SIDES):
        for j in OTHERS:
            sent(own_q, qz_ss.at[yy, j])
    sent(hid_q.at[:, c], qs_ss.at[0])
    for q in range(ROWS):
        ref = doc(me, q)
        for zs in range(4):
            sent(ref, dy_ss.at[zs, q])

            @pl.when(jnp.logical_and(zs >= z, z > 0))
            def _():
                sent(ref, dl_ss.at[zs, q])

            @pl.when(jnp.logical_and(zs <= z, z < 3))
            def _():
                sent(ref, dr_ss.at[zs, q])
        for p in range(n_pair):
            sent(ref, ds_ss.at[p, q])

    mean_q = jnp.mean(rep_q[...], **DOWN)
    mean_d = jnp.mean(rep_d[...], **DOWN)
    reg = (lam_q * jnp.sum(mean_q * mean_q, **ACROSS)
           + lam_d * jnp.sum(mean_d * mean_d, **ACROSS))
    hq = n_q // 2
    part_s = lax.dot_general(rep_q[...], rep_d[...], NT_DIMS, precision=HIGHEST, preferred_element_type=F32)
    s_a[quad, 0:hq, 0:n_d] = part_s[0:hq]
    s_a[quad, 0:hq, n_d:128] = part_s[hq:n_q]
    s_a[quad, hq:hq + 8, :] = jnp.broadcast_to(reg, (8, 128))
    for j in OTHERS:
        remote(s_a.at[quad], s_a.at[quad], sa_ss.at[j], sa_rs.at[quad], plane[j - 1]).start()
    for i in range(NDEV):
        info = meta[i // N_Z, (i // SIDES) % SIDES, i % SIDES].astype(F32)
        pos_s[ROWS * i:ROWS * (i + 1), :] = info[PAIR:3 * ROWS, 0:128]
    for j in OTHERS:
        src = (quad + j) % 4
        got(s_a.at[src], sa_rs.at[src])
    s_b[z] = s_a[0] + s_a[1] + s_a[2] + s_a[3]
    for j in OTHERS:
        remote(s_b.at[z], s_b.at[z], sb_ss.at[j], sb_rs.at[z], line[j - 1]).start()
    for j in OTHERS:
        src = (z + j) % N_Z
        got(s_b.at[src], sb_rs.at[src])
    total = s_b[0] + s_b[1] + s_b[2] + s_b[3]
    scores = jnp.concatenate([total[0:hq, 0:n_d], total[0:hq, n_d:128]], axis=0)
    top = jnp.max(scores, **ACROSS)
    log_norm = top + jnp.log(jnp.sum(jnp.exp(scores - top), **ACROSS))
    lane = lax.broadcasted_iota(jnp.int32, (n_q, n_d), 1).astype(F32)
    target = (pos_s[:, 0:n_d] == lane).astype(F32)
    picked = jnp.sum(target * scores, **ACROSS)
    cross = jnp.sum(log_norm - picked, **DOWN) / n_q
    loss[...] = cross + total[hq:hq + 1, 0:1]
    grad_s = (jnp.exp(scores - log_norm) - target) / n_q

    @pl.loop(0, tiles)
    def _(n):
        cols = tile(n)
        rep_qn, rep_dn = rep_q[:, cols], rep_d[:, cols]
        back_q = lax.dot_general(
            grad_s, rep_dn, (((1,), (0,)), ((), ())), precision=HIGHEST, preferred_element_type=F32
        ) + (2.0 * lam_q / n_q) * jnp.mean(rep_qn, **DOWN)
        back_d = lax.dot_general(
            grad_s, rep_qn, TN_DIMS, precision=HIGHEST, preferred_element_type=F32
        ) + (2.0 * lam_d / n_d) * jnp.mean(rep_dn, **DOWN)
        rep_q[:, cols] = back_q
        rep_d[:, cols] = back_d

    db[...] = jnp.zeros_like(db)
    for j in OTHERS:
        sent(s_a.at[0], sa_ss.at[j])
        sent(s_b.at[0], sb_ss.at[j])

    grad_q, grad_d = rep_q, rep_d
    bufs = (low, wv)

    def pair_of(j):
        end, odd, some = j // 7, j % 2, (j + 6) // 7
        other = odd * (1 - end) + (1 - odd) * (1 - some)
        k = odd * ((7 - j) // 2 - 1 + end) + (1 - odd) * (4 - j // 2 - (1 - some))
        zs = order(k)
        return other, zs, spot(zs, y) + other * (1 - 2 * y)

    def hidden_grad(rows, buf, store, beside):
        @pl.loop(0, hidden // TILE)
        def _(t):
            out = jnp.zeros((rows, TILE), F32)
            for n in range(tiles):
                r, l = w_block(n, t * TILE, TILE)
                out = out + jnp.dot(buf[0:rows, n * TILE:(n + 1) * TILE], dw[r, l],
                                    preferred_element_type=F32)
            store(tile(t), out.astype(BF16))
            beside(t)

    def docs_gate(p, buf, n):
        cols = tile(n)
        total_b = jnp.zeros((1, TILE), F32)
        for d in range(PAIR):
            gz = (grad_d[pl.ds(PAIR * p + d, 1), cols]
                  * gate_d[pl.ds(p * pair_rows + d_len * d, d_len), cols])
            total_b = total_b + jnp.sum(gz, **DOWN)
            buf[d_len * d:d_len * (d + 1), cols] = gz.astype(BF16)
        db[:, cols] += total_b

    def docs_hidden(slot, beside):
        def store(hrows, out):
            part[slot, :, :, hrows] = out.reshape(2, rd, TILE)
        hidden_grad(pair_rows, bufs[slot], store, beside)

    def two_queries(q, cols):
        return jnp.concatenate(
            [grad_q[q + i:q + i + 1, cols] * gate_q[q_len * (q + i):q_len * (q + i + 1), cols]
             for i in range(SIDES)], axis=0)

    def queries_back():
        buf = bufs[0]

        @pl.loop(0, tiles)
        def _(n):
            cols = tile(n)
            total_b = jnp.zeros((1, TILE), F32)
            for q in range(0, n_q, 2):
                gz = two_queries(q, cols)
                total_b = total_b + jnp.sum(gz, **DOWN)
                buf[q_len * q:q_len * (q + 2), cols] = gz.astype(BF16)
            db[:, cols] += total_b

        chip_sum(0)

        def store(hrows, out):
            part_q[:, :, :, hrows] = out.reshape(n_pair, 2, rq, TILE)
        hidden_grad(NDEV * rq, buf, store, lambda t: None)
        remote(part_q.at[:, 1 - c], hid_q.at[:, 1], cs_ss.at[0], cs_rs.at[0], sib).start()

    def queries_chip():
        got(hid_q.at[:, 1], cs_rs.at[0])

        @pl.loop(0, n_pair)
        def _(p):
            hid_q[p, 0] = (part_q[p, c].astype(F32) + hid_q[p, 1].astype(F32)).astype(BF16)
        for j in OTHERS:
            zs = (z + j) % N_Z
            remote(hid_q.at[pl.ds(2 * zs, 2), 0], in_qz.at[z], cz_ss.at[j], cz_rs.at[z],
                   (me + 4 * j) % NDEV).start()

    def queries_line():
        for j in OTHERS:
            src = (z + j) % N_Z
            got(in_qz.at[src], cz_rs.at[src])
        for yy in range(SIDES):
            p = spot(z, yy)
            s = hid_q[p, 0].astype(F32)
            for j in OTHERS:
                s = s + in_qz[(z + j) % N_Z, yy].astype(F32)
            hid_q[p, 0] = s.astype(BF16)
        remote(hid_q.at[spot(z, 1 - y), 0], in_qy, cy_ss.at[0], cy_rs.at[0], over_y).start()

    def queries_end():
        got(in_qy, cy_rs.at[0])
        dhq[...] = (hid_q[spot(z, y), 0].astype(F32) + in_qy[...].astype(F32)).astype(BF16)

    def chip_sum(j):
        other, zs, p = pair_of(j)
        slot = j % 2
        got(hid_d.at[n_pair + p], bs_rs.at[p])

        @pl.loop(0, rd // 32)
        def _(t):
            r = pl.ds(pl.multiple_of(t * 32, 32), 32)
            hid_d[p, r] = (part[slot, c, r].astype(F32) + hid_d[n_pair + p, r].astype(F32)).astype(BF16)

        @pl.when(other == 1)
        def _():
            for h in range(SIDES):
                r = pl.ds(h * half, half)
                remote(hid_d.at[p, r], in_y.at[zs, r], by_ss.at[zs, h], by_rs.at[zs, h], over_y).start()

    def line_step(e):
        k, h = 3 - e // 2, e % 2
        d = order(k)
        p = spot(d, y)
        r = pl.ds(h * half, half)
        from_left = jnp.logical_and(z > 0, d >= z)
        from_right = jnp.logical_and(z < 3, d <= z)
        left_slot = jnp.maximum(d - 1, 0)
        right_slot = jnp.minimum(d, 2)
        got(in_y.at[d, r], by_rs.at[d, h])

        @pl.when(from_left)
        def _():
            got(in_l.at[left_slot, r], bl_rs.at[d, h])

        @pl.when(from_right)
        def _():
            got(in_r.at[right_slot, r], br_rs.at[d, h])

        def add(*terms):
            @pl.loop(0, half // 16)
            def _(i):
                q = pl.ds(pl.multiple_of(h * half + i * 16, 16), 16)
                s = hid_d[p, q].astype(F32) + in_y[d, q].astype(F32)
                for ref, slot in terms:
                    s = s + ref[slot, q].astype(F32)
                if k == 0:
                    dhd[q] = s.astype(BF16)
                else:
                    hid_d[p, q] = s.astype(BF16)

        both = jnp.logical_and(from_left, from_right)
        pl.when(both)(lambda: add((in_l, left_slot), (in_r, right_slot)))
        pl.when(jnp.logical_and(from_left, jnp.logical_not(from_right)))(lambda: add((in_l, left_slot)))
        pl.when(jnp.logical_and(from_right, jnp.logical_not(from_left)))(lambda: add((in_r, right_slot)))
        pl.when(jnp.logical_not(jnp.logical_or(from_left, from_right)))(lambda: add())
        if k > 0:
            @pl.when(d < z)
            def _():
                remote(hid_d.at[p, r], in_r.at[jnp.minimum(d, 2), r], bl_ss.at[d, h], br_rs.at[d, h], left).start()

            @pl.when(d > z)
            def _():
                remote(hid_d.at[p, r], in_l.at[jnp.maximum(d - 1, 0), r], br_ss.at[d, h], bl_rs.at[d, h], right).start()

    depth = NDEV * rq
    blocks = (all_d + depth) // depth
    steps = max(hidden // 512, 1)

    def weight_gate(n, buf, m):
        cols = tile(n)
        share = n_d // steps

        for i in range(share):
            d = m * share + i
            r = pl.ds(pl.multiple_of(d * d_len, 16), d_len)
            gz = (grad_d[pl.ds(d, 1), cols] * gate_d[r, cols]).astype(BF16)
            for piece in range(0, d_len, 16):
                at = m * share * d_len + i * d_len + piece
                blk, row = at // depth, at % depth
                buf[pl.ds(pl.multiple_of(row, 16), 16), tile(blk)] = gz[piece:piece + 16]

    def weight_gate_q(n, buf):
        cols = tile(n)
        for q in range(0, n_q, 2):
            buf[q_len * q:q_len * (q + 2), (blocks - 1) * TILE:blocks * TILE] = two_queries(q, cols).astype(BF16)

    def weight_grad(n, slot, ahead):
        cols = tile(n)
        size = hidden // steps
        for m in range(steps):
            r = slice(m * size, (m + 1) * size)
            out = jnp.zeros((size, TILE), F32)
            for i in range(blocks):
                out = out + jnp.dot(hid_t[r, i * depth:(i + 1) * depth],
                                    bufs[slot][0:depth, i * TILE:(i + 1) * TILE], preferred_element_type=F32)
            dw[r, cols] = out.astype(BF16)
            pltpu.make_async_copy(dw.at[r, cols], dw_out.at[r, cols], out_sem.at[m, n]).start()
            weight_gate(ahead, bufs[1 - slot], m)
        weight_gate_q(ahead, bufs[1 - slot])

    pair_tiles = tiles // (hidden // TILE)

    def gate_next(j, slot, t):
        _, _, p = pair_of(j)
        for i in range(pair_tiles):
            docs_gate(p, bufs[slot], t * pair_tiles + i)

    @pl.loop(0, hidden // TILE)
    def _(t):
        gate_next(0, 0, t)

    @pl.loop(0, 9 + tiles)
    def _(u):
        is_pair = jnp.logical_and(u < 9, u != 1)
        j = u - jnp.minimum(u, 1)
        for slot in range(SIDES):
            @pl.when(jnp.logical_and(is_pair, j % 2 == slot))
            def _():
                _, _, p = pair_of(j)

                @pl.when(j >= 2)
                def _():
                    sent(part.at[0, 0], bs_ss.at[slot])
                if slot == 0:
                    docs_hidden(0, lambda t: gate_next(j + 1, 1, t))
                else:
                    @pl.when(j < 7)
                    def _():
                        docs_hidden(1, lambda t: gate_next(j + 1, 0, t))

                    @pl.when(j == 7)
                    def _():
                        docs_hidden(1, lambda t: None)
                remote(part.at[slot, 1 - c], hid_d.at[n_pair + p], bs_ss.at[slot], bs_rs.at[p], sib).start()

                @pl.when(j >= 2)
                def _():
                    chip_sum(j - 1)

        @pl.when(u == 1)
        def _():
            queries_back()

        @pl.when(u == 2)
        def _():
            queries_chip()

        @pl.when(u == 9)
        def _():
            for m in range(steps):
                weight_gate(0, bufs[1], m)
            weight_gate_q(0, bufs[1])
            chip_sum(7)

        for slot in range(SIDES):
            @pl.when(jnp.logical_and(u >= 9, u % 2 == slot))
            def _():
                n = u - 9
                weight_grad(n, slot, jnp.minimum(n + 1, tiles - 1))

        @pl.when(u == 13)
        def _():
            queries_line()

        for e in range(8):
            at = END_AT[e] * (1 - mid) + MID_AT[e] * mid

            @pl.when(u == jnp.minimum(at, 8 + tiles))
            def _():
                line_step(e)

    queries_end()
    for m in range(steps):
        for n in range(tiles):
            r = slice(m * (hidden // steps), (m + 1) * (hidden // steps))
            l = slice(n * TILE, (n + 1) * TILE)
            pltpu.make_async_copy(dw.at[r, l], dw_out.at[r, l], out_sem.at[m, n]).wait()
    for slot in range(SIDES):
        sent(part.at[0, 0], bs_ss.at[slot])
    sent(part_q.at[:, 0], cs_ss.at[0])
    for j in OTHERS:
        sent(in_qz.at[0], cz_ss.at[j])
    sent(in_qy, cy_ss.at[0])
    for h in range(SIDES):
        for zs in range(4):
            ref = in_y.at[0, pl.ds(0, half)]
            sent(ref, by_ss.at[zs, h])

            @pl.when(zs < z)
            def _():
                sent(ref, bl_ss.at[zs, h])

            @pl.when(zs > z)
            def _():
                sent(ref, br_ss.at[zs, h])


def hand_over(dw, db, dhd, dhq, dw_out, db_out, dhd_out, dhq_out, buf_w, buf_b, buf_d, buf_q, read, write):
    steps = 8
    rows = dw.shape[0] // steps
    moves = [(dw.at[pl.ds(i * rows, rows)], buf_w.at[pl.ds(i * rows, rows)], dw_out.at[pl.ds(i * rows, rows)])
             for i in range(steps)]
    moves += [(dhd, buf_d, dhd_out), (dhq, buf_q, dhq_out), (db, buf_b, db_out)]
    for i, (src, buf, dst) in enumerate(moves):
        pltpu.make_async_copy(src, buf, read.at[i]).start()
    for i, (src, buf, dst) in enumerate(moves):
        pltpu.make_async_copy(src, buf, read.at[i]).wait()
        pltpu.make_async_copy(buf, dst, write.at[i]).start()
    for i, (src, buf, dst) in enumerate(moves):
        pltpu.make_async_copy(buf, dst, write.at[i]).wait()


def solution(mesh):
    group_size = mesh.shape['tp']

    def device_step(query_hidden, doc_hidden, query_mask, doc_mask, positives, head_weight, head_bias):
        hidden, cols = head_weight.shape
        vocab_size = cols * group_size
        q_len = query_hidden.shape[1]
        d_len = doc_hidden.shape[1]
        lam_q = math.sqrt(d_len) / (4.0 * math.sqrt(vocab_size) * q_len)
        lam_d = q_len / (4.0 * math.sqrt(vocab_size) * d_len ** 1.5)
        rd, rq = ROWS * d_len, ROWS * q_len
        n_q = NDEV * ROWS
        all_d, all_q = NDEV * rd, NDEV * rq
        pair_rows = SIDES * rd
        vmem = pl.BlockSpec(memory_space=pltpu.VMEM)
        hbm = pl.BlockSpec(memory_space=pl.ANY)
        dma = pltpu.SemaphoreType.DMA
        one, few = dma((1,)), dma((NDEV // SIDES,))
        out_y, in_z = dma((SIDES, N_Z)), dma((N_Z, SIDES))
        by_doc, all_docs, by_half = dma((N_Z, ROWS)), dma((NDEV // SIDES, ROWS)), dma((N_Z, SIDES))
        out = pl.pallas_call(
            functools.partial(kernel, d_len, q_len, lam_q, lam_d),
            out_shape=[
                jax.ShapeDtypeStruct((1, 1), F32),
                jax.ShapeDtypeStruct((hidden, cols), BF16),
                jax.ShapeDtypeStruct((1, cols), F32),
                jax.ShapeDtypeStruct((rd, hidden), BF16),
                jax.ShapeDtypeStruct((rq, hidden), BF16),
            ],
            in_specs=[hbm, hbm, vmem, vmem, pl.BlockSpec(memory_space=pltpu.SMEM), hbm, vmem],
            out_specs=[vmem, hbm, vmem, vmem, vmem],
            scratch_shapes=[
                pltpu.VMEM((NDEV, rd, hidden), BF16),
                pltpu.VMEM((NDEV // 2, 2, rq, hidden), BF16),
                pltpu.VMEM((N_Z, SIDES, SIDES, 16, TILE), BF16),
                pltpu.VMEM((2, 16, TILE), BF16),
                pltpu.VMEM((hidden, cols), BF16),
                pltpu.VMEM((hidden, cols), BF16),
                pltpu.VMEM((hidden, all_d + all_q), BF16),
                pltpu.VMEM((all_d, cols), F32),
                pltpu.VMEM((all_q, cols), F32),
                pltpu.VMEM((n_q, cols), F32),
                pltpu.VMEM((n_q, cols), F32),
                pltpu.VMEM((max(all_q, pair_rows), cols), BF16),
                pltpu.VMEM((2, 2, rd, hidden), BF16),
                pltpu.VMEM((NDEV // 2, 2, rq, hidden), BF16),
                pltpu.VMEM((4, rd, hidden), BF16),
                pltpu.VMEM((3, rd, hidden), BF16),
                pltpu.VMEM((3, rd, hidden), BF16),
                pltpu.VMEM((4, 2, rq, hidden), BF16),
                pltpu.VMEM((rq, hidden), BF16),
                pltpu.VMEM((max(all_q, pair_rows), TILE), F32),
                pltpu.VMEM((max(all_q, pair_rows), TILE), F32),
                pltpu.VMEM((n_q, 128), F32),
                pltpu.VMEM((4, n_q // 2 + 8, 128), F32),
                pltpu.VMEM((4, n_q // 2 + 8, 128), F32),
                few, dma((max(hidden // 512, 1), cols // TILE)), few, few, one, one, out_y, in_z, one, one,
                by_doc, by_doc, by_doc, by_doc, by_doc, all_docs, all_docs,
                few, few, few, few,
                few, few, by_half, by_half, by_half, by_half, by_half, by_half,
                one, one, few, few, one, one,
            ],
            compiler_params=pltpu.CompilerParams(
                collective_id=0, has_side_effects=True, vmem_limit_bytes=67043328),
        )(doc_hidden.reshape(rd, hidden), query_hidden.reshape(rq, hidden), doc_mask, query_mask, positives,
          head_weight, head_bias)
        total_loss = out[0]
        grad_weight, grad_bias, grad_doc, grad_query = pl.pallas_call(
            hand_over,
            out_shape=[jax.ShapeDtypeStruct(x.shape, x.dtype) for x in out[1:]],
            in_specs=[hbm] * 4,
            out_specs=[hbm] * 4,
            scratch_shapes=[pltpu.VMEM(x.shape, x.dtype) for x in out[1:]] + [dma((11,)), dma((11,))],
        )(*out[1:])
        return (total_loss.reshape(1), grad_weight, grad_bias,
                grad_query.reshape(query_hidden.shape), grad_doc.reshape(doc_hidden.shape))

    batch_rows = P(('dp', 'tp'), None, None)
    batch_masks = P(('dp', 'tp'), None)
    return jax.shard_map(device_step, mesh=mesh, in_specs=(batch_rows, batch_rows, batch_masks, batch_masks, P(('dp', 'tp')), P(None, 'tp'), P(None, 'tp')), out_specs=(P('dp'), P('dp', 'tp'), P('dp', 'tp'), batch_rows, batch_rows), check_vma=False)
```

time: 162 us -> 135 us (0.83)
  Pallas kernels: 152 us -> 133 us
  local copies, waits for them, and re-layouts: 6.83 us -> 0 us
    pallas_call x1, Pallas kernels: 152 us -> 129 us  [device_step(): pl.pallas_call(functools.partial(kernel, d_len, q_len, lam_q, lam_d), out...]
    unnamed x10 -> x0, local copies, waits for them, and re-layouts: 6.83 us -> none
    pallas_call x0 -> x1, Pallas kernels: none -> 4.01 us  [device_step(): pl.pallas_call(hand_over, out_shape=[jax.ShapeDtypeStruct(x.shape, x.dtyp...]
where the time goes in v2:
time: 135 us
  Pallas kernels  133 us (99%)
  between operations  2.33 us (2%)
    pallas_call x1, Pallas kernels, device_step(): pl.pallas_call(functools.partial(kernel, d_len, q_len, lam_q, lam_d), out...  129 us
    pallas_call x1, Pallas kernels, device_step(): pl.pallas_call(hand_over, out_shape=[jax.ShapeDtypeStruct(x.shape, x.dtyp...  4.01 us

profile of v2, /device:TPU:0, one launch (start us, length us, event | category | flops | bytes accessed | tf_op | source)
XLA Modules:
  0.0 135.0 jit_solution(4872175317544966805)
XLA Ops:
  0.6 128.6 %shard_map.110 = (f32[1,1]{1,0:T(1,128)}, bf16[1024,2048]{1,0:T(8,128)(2,1)}, f32[1,2048]{1,0:T(1,128)}, bf16[192,1024]{1,0:T(8,128)(2,1)}, bf16[32,1024]{1,0:T(8,128)(2,1)}) custom-call(bf16[192,1024]{1,0:T(8,128)(2,1)} %bitcast.5, bf16[32,1024]{1,0:T(8,128)(2,1)} %bitcast.6, s32[4,48]{1,0:T(4,128)} %md.1, s32[4,8]{1,0:T(4,128)} %mq.1, s32[4]{0:T(128)} %pos.1, ...), custom_call_target="tpu_custom_call" | custom-call | tf_op jit(solution)/shard_map/pallas_call | solution.py:735
  129.3 4.0 %shard_map.111 = (bf16[1024,2048]{1,0:T(8,128)(2,1)}, f32[1,2048]{1,0:T(1,128)}, bf16[192,1024]{1,0:T(8,128)(2,1)}, bf16[32,1024]{1,0:T(8,128)(2,1)}) custom-call(bf16[1024,2048]{1,0:T(8,128)(2,1)} %get-tuple-element.15.dw, f32[1,2048]{1,0:T(1,128)} %get-tuple-element.16.db, bf16[192,1024]{1,0:T(8,128)(2,1)} %get-tuple-element.17.dhd, ...), custom_call_target="tpu_custom_call" | custom-call | tf_op jit(solution)/shard_map/pallas_call | solution.py:782
